TPU v7x, 128 devices: a whole 4x4x4 slice. The times are simulated.
128 devices in a mesh: row: 8 (over y, core), col: 16 (over x, z).
Axes of the slice: x: 4, y: 4, z: 4, core: 2. Of those that a mesh axis runs over, the one named last changes fastest.
Arguments:
- matrix_in: float32 [4, 4096, 2, 8192], P(None, 'row', None, 'col'), as said below
- panel_start: int32 [1], replicated, may hold values from 0 to 29
Outputs:
- matrix_out: float32 [4, 4096, 2, 8192], P(None, 'row', None, 'col')
Inputs may be any that keep to these rules, and one draw needn't show every extreme that they name: matrix_in is symmetric and positive definite.
All inputs are finite; a program needn't handle non-finite values.
Results may differ from a plain program's by a relative error of at most 0.0001.
Values sent between devices are 32-bit elements.
No kernel may reach another device: no remote copies, remote signals or barrier semaphores. Data moves between devices by JAX's collectives and lax.ppermute only.
A program may use at most 128 MiB of HBM per device.

v0:
```python
import jax
import jax.numpy as jnp
from jax import lax
from jax.sharding import PartitionSpec as P


def picked(x, axis, root):
    return lax.dynamic_index_in_dim(lax.all_gather(x, axis), root, 0, keepdims=False)


def from_root(value, axis, source):
    kept = jnp.where(lax.axis_index(axis) == source, value, 0).astype(value.dtype)
    return lax.psum(kept, axis)


def padded_to(lines, length):
    spare = -lines.shape[0] % length
    if not spare:
        return lines
    return jnp.concatenate([lines, jnp.zeros((spare, *lines.shape[1:]), lines.dtype)])


def broadcast_by_parts(x, axis, root):
    lines = jnp.where(lax.axis_index(axis) == root, x, jnp.zeros_like(x)).reshape(
        -1, *x.shape[1:][-1:]
    )
    padded = padded_to(lines, lax.axis_size(axis))
    own = lax.psum_scatter(padded, axis, scatter_dimension=0, tiled=True)
    return lax.all_gather(own, axis, axis=0, tiled=True)[: len(lines)].reshape(x.shape)


def update(matrix, rows_part, cols_part):
    loc_rows, width, _unused_a = rows_part.shape
    loc_cols = cols_part.shape[0]
    left_panel = rows_part.reshape(loc_rows * width, width)
    right_panel = cols_part.reshape(loc_cols * width, width)
    product = lax.dot_general(
        left_panel,
        right_panel,
        (((1,), (1,)), ((), ())),
        precision=lax.Precision.HIGHEST,
        preferred_element_type=jnp.float32,
    )
    return matrix - product.reshape(loc_rows, width, loc_cols, width)


def factor_panel(matrix, panel):
    rows_dev = lax.axis_size("row")
    cols_dev = lax.axis_size("col")
    my_row = lax.axis_index("row")
    my_col = lax.axis_index("col")
    loc_rows, width, loc_cols, _unused_b = matrix.shape
    row_blocks = jnp.arange(loc_rows, dtype=jnp.int32) * rows_dev + my_row
    col_local = panel // cols_dev
    row_local = panel // rows_dev
    owner_row = panel % rows_dev
    owner_col = panel % cols_dev
    column_strip = lax.dynamic_index_in_dim(matrix, col_local, 2, keepdims=False)
    diag_raw = lax.dynamic_index_in_dim(column_strip, row_local, 0, keepdims=False)
    factor = picked(jnp.linalg.cholesky(diag_raw), "row", owner_row)
    flat_rows = column_strip.reshape(loc_rows * width, width)
    solved = jax.scipy.linalg.solve_triangular(factor, flat_rows.T, lower=True).T
    solved = solved.reshape(loc_rows, width, width)
    below_panel = (row_blocks > panel)[:, None, None]
    on_panel = (row_blocks == panel)[:, None, None]
    rows_local = jnp.where(below_panel, solved, jnp.float32(0.0))
    rows_part = from_root(rows_local, "col", owner_col)
    new_strip = jnp.where(below_panel, solved, column_strip)
    new_strip = jnp.where(on_panel, factor[None, :, :], new_strip)
    written = jnp.where(my_col == owner_col, new_strip, column_strip)
    matrix = lax.dynamic_update_index_in_dim(matrix, written, col_local, 2)
    stride_ratio = cols_dev // rows_dev
    source_row = my_col % rows_dev
    offset_pick = my_col // rows_dev
    received = broadcast_by_parts(rows_part, "row", source_row)
    grouped = received.reshape(loc_cols, stride_ratio, width, width)
    cols_part = lax.dynamic_index_in_dim(grouped, offset_pick, 1, keepdims=False)
    return (rows_part, cols_part, matrix)


def per_device(matrix_in, panel_start):
    first_panel = panel_start[0]
    matrix = matrix_in
    cols_dev = lax.axis_size("col")
    loc_rows, width, loc_cols, _unused_c = matrix.shape
    rows_first, cols_first, matrix = factor_panel(matrix, first_panel)
    next_panel = first_panel + 1
    col_next = next_panel // cols_dev
    next_strip = lax.dynamic_index_in_dim(matrix, col_next, 2, keepdims=False)
    next_piece = lax.dynamic_index_in_dim(cols_first, col_next, 0, keepdims=False)
    left_panel = rows_first.reshape(loc_rows * width, width)
    strip_product = lax.dot_general(
        left_panel,
        next_piece,
        (((1,), (1,)), ((), ())),
        precision=lax.Precision.HIGHEST,
        preferred_element_type=jnp.float32,
    )
    next_strip = next_strip - strip_product.reshape(loc_rows, width, width)
    matrix = lax.dynamic_update_index_in_dim(matrix, next_strip, col_next, 2)
    rows_second, cols_second, matrix = factor_panel(matrix, next_panel)
    skipped = (jnp.arange(loc_cols, dtype=jnp.int32) == col_next)[:, None, None]
    cols_rest = jnp.where(skipped, jnp.float32(0.0), cols_first)
    matrix = update(matrix, rows_first, cols_rest)
    matrix = update(matrix, rows_second, cols_second)
    return matrix


def solution(mesh):
    return jax.shard_map(
        per_device,
        mesh=mesh,
        in_specs=(P(None, "row", None, "col"), P()),
        out_specs=P(None, "row", None, "col"),
        check_vma=False,
    )
```

profile of v0, /device:TPU:1, one launch (start us, length us, event | category | flops | bytes accessed | tf_op | source)
XLA Modules:
  0.0 873.0 jit_solution(14277893120988400959)
XLA Ops:
  7.2 2.5 constant_dynamic-slice_fusion.6
  11.3 11.7 %cholesky.286 = f32[128,128]{1,0:T(8,128)S(1)} custom-call(f32[128,128]{1,0:T(8,128)S(1)} %cholesky.426), custom_call_target="Cholesky" | custom-call | tf_op jit(solution)/shard_map/jit(cholesky)/cholesky | solution.py:60
  23.1 9.8 %custom-call.27 = f32[1,128,128]{1,2,0:T(8,128)S(1)} custom-call(f32[1,128,128]{2,1,0:T(8,128)S(1)} %get-tuple-element.66), custom_call_target="InvertDiagBlocksLowerTriangular" | custom-call | tf_op jit(solution)/shard_map/jit(cholesky)/cholesky | solution.py:60
  33.7 11.7 %cholesky.305 = f32[128,128]{1,0:T(8,128)S(1)} custom-call(f32[128,128]{1,0:T(8,128)S(1)} %cholesky.430), custom_call_target="Cholesky" | custom-call | tf_op jit(solution)/shard_map/jit(cholesky)/cholesky | solution.py:60
  45.4 10.0 %custom-call.28 = f32[1,128,128]{1,2,0:T(8,128)S(1)} custom-call(f32[1,128,128]{2,1,0:T(8,128)S(1)} %get-tuple-element.63), custom_call_target="InvertDiagBlocksLowerTriangular" | custom-call | tf_op jit(solution)/shard_map/jit(cholesky)/cholesky | solution.py:60
  56.1 11.7 %cholesky.326 = f32[128,128]{1,0:T(8,128)S(1)} custom-call(f32[128,128]{1,0:T(8,128)S(1)} %cholesky.435), custom_call_target="Cholesky" | custom-call | tf_op jit(solution)/shard_map/jit(cholesky)/cholesky | solution.py:60
  68.5 9.8 %custom-call.29 = f32[1,128,128]{1,2,0:T(8,128)S(1)} custom-call(f32[1,128,128]{2,1,0:T(8,128)S(1)} %get-tuple-element.60), custom_call_target="InvertDiagBlocksLowerTriangular" | custom-call | tf_op jit(solution)/shard_map/jit(cholesky)/cholesky | solution.py:60
  78.9 11.7 %cholesky.343 = f32[128,128]{1,0:T(8,128)S(1)} custom-call(f32[128,128]{1,0:T(8,128)S(1)} %convolution_subtract_fusion.9), custom_call_target="Cholesky" | custom-call | tf_op jit(solution)/shard_map/jit(cholesky)/cholesky | solution.py:60
  96.1 8.3 copy.7
  104.4 4.6 constant_dynamic-slice_fusion.5
  109.0 40.4 %all-gather.11.cloned.1.call-done = f32[4096,512]{1,0:T(8,128)} async-done(((f32[512,512]{1,0:T(8,128)}), f32[4096,512]{1,0:T(8,128)}) %all-gather.11.cloned.1.call-update) | async-done | bytes 8388624 | tf_op jit(solution)/shard_map/all_gather | solution.py:8
  151.0 8.2 while.4
  159.2 39.7 %custom-call.30 = f32[4,128,128]{1,2,0:T(8,128)S(1)} custom-call(f32[4,128,128]{2,1,0:T(8,128)S(1)} %get-tuple-element.21), custom_call_target="InvertDiagBlocksLowerTriangular" | custom-call | tf_op jit(solution)/shard_map/jit(_solve_triangular)/triangular_solve | solution.py:62
  201.3 3.0 convolution_subtract_fusion.3
  205.5 3.5 convolution_subtract_fusion.1
  210.1 5.5 fusion.19
  216.7 2.5 maximum_bitcast_fusion
  219.2 5.3 copy.19
  224.5 4.9 select_select_fusion.1
  229.5 103.3 %all-reduce.4.cloned.1.call-done = f32[4,512,512]{2,1,0:T(8,128)} async-done(((f32[4,512,512]{2,1,0:T(8,128)}), f32[4,512,512]{2,1,0:T(8,128)}) %all-reduce.4.cloned.1.call-update) | async-done | bytes 4194320 | tf_op jit(solution)/shard_map/psum | solution.py:13
  335.3 36.9 %reduce-scatter.3.cloned.1.call-done = f32[256,512]{1,0:T(8,128)} async-done(((f32[2048,512]{1,0:T(8,128)}), f32[256,512]{1,0:T(8,128)}) %reduce-scatter.3.cloned.1.call-update) | async-done | bytes 524304 | tf_op jit(solution)/shard_map/reduce_scatter | solution.py:28
  372.3 6.8 select_dynamic-update-slice_fusion.1
  379.2 4.6 constant_dynamic-slice_fusion.4
  383.7 24.3 %all-gather.7.cloned.1.call-done = f32[2048,512]{1,0:T(8,128)} async-done(((f32[256,512]{1,0:T(8,128)}), f32[2048,512]{1,0:T(8,128)}) %all-gather.7.cloned.1.call-update) | async-done | bytes 4194320 | tf_op jit(solution)/shard_map/all_gather | solution.py:29
  408.0 11.0 %bitcast_dynamic-update-slice_fusion.2 = f32[4,512,2,512]{3,1,2,0:T(8,128)} fusion(f32[4,512,2,512]{3,1,2,0:T(8,128)} %select_dynamic-update-slice_fusion.1, s32[]{:T(128)S(6)} %select_n.178, f32[4,512,1,512]{3,1,2,0:T(8,128)} %constant_dynamic-slice_fusion.4, f32[4,512,512]{2,1,0:T(8,128)} %all-reduce.4.cloned.1.call-done, ...), kind=kOutput, calls=%fused_computation.11 | convolution fusion | flops 6443499520 | bytes 13631500 | tf_op jit(solution)/shard_map/dot_general | solution.py:92
  422.1 11.7 %cholesky.358 = f32[128,128]{1,0:T(8,128)S(1)} custom-call(f32[128,128]{1,0:T(8,128)S(1)} %cholesky.439), custom_call_target="Cholesky" | custom-call | tf_op jit(solution)/shard_map/jit(cholesky)/cholesky | solution.py:60
  434.5 9.8 %custom-call.31 = f32[1,128,128]{1,2,0:T(8,128)S(1)} custom-call(f32[1,128,128]{2,1,0:T(8,128)S(1)} %get-tuple-element.56), custom_call_target="InvertDiagBlocksLowerTriangular" | custom-call | tf_op jit(solution)/shard_map/jit(cholesky)/cholesky | solution.py:60
  445.1 11.7 %cholesky.377 = f32[128,128]{1,0:T(8,128)S(1)} custom-call(f32[128,128]{1,0:T(8,128)S(1)} %cholesky.443), custom_call_target="Cholesky" | custom-call | tf_op jit(solution)/shard_map/jit(cholesky)/cholesky | solution.py:60
  457.6 10.2 %custom-call.32 = f32[1,128,128]{1,2,0:T(8,128)S(1)} custom-call(f32[1,128,128]{2,1,0:T(8,128)S(1)} %get-tuple-element.53), custom_call_target="InvertDiagBlocksLowerTriangular" | custom-call | tf_op jit(solution)/shard_map/jit(cholesky)/cholesky | solution.py:60
  468.5 11.7 %cholesky.398 = f32[128,128]{1,0:T(8,128)S(1)} custom-call(f32[128,128]{1,0:T(8,128)S(1)} %cholesky.448), custom_call_target="Cholesky" | custom-call | tf_op jit(solution)/shard_map/jit(cholesky)/cholesky | solution.py:60
  480.9 9.8 %custom-call.33 = f32[1,128,128]{1,2,0:T(8,128)S(1)} custom-call(f32[1,128,128]{2,1,0:T(8,128)S(1)} %get-tuple-element.50), custom_call_target="InvertDiagBlocksLowerTriangular" | custom-call | tf_op jit(solution)/shard_map/jit(cholesky)/cholesky | solution.py:60
  491.3 11.7 %cholesky.415 = f32[128,128]{1,0:T(8,128)S(1)} custom-call(f32[128,128]{1,0:T(8,128)S(1)} %convolution_subtract_fusion.8), custom_call_target="Cholesky" | custom-call | tf_op jit(solution)/shard_map/jit(cholesky)/cholesky | solution.py:60
  507.6 4.6 constant_dynamic-slice_fusion.2
  512.2 45.1 %all-gather.13.cloned.1.call-done = f32[4096,512]{1,0:T(8,128)} async-done(((f32[512,512]{1,0:T(8,128)}), f32[4096,512]{1,0:T(8,128)}) %all-gather.13.cloned.1.call-update) | async-done | bytes 8388624 | tf_op jit(solution)/shard_map/all_gather | solution.py:8
  558.8 7.9 while.5
  566.7 39.3 %custom-call.34 = f32[4,128,128]{1,2,0:T(8,128)S(1)} custom-call(f32[4,128,128]{2,1,0:T(8,128)S(1)} %get-tuple-element.22), custom_call_target="InvertDiagBlocksLowerTriangular" | custom-call | tf_op jit(solution)/shard_map/jit(_solve_triangular)/triangular_solve | solution.py:62
  608.5 3.0 convolution_subtract_fusion.2
  612.6 3.5 convolution_subtract_fusion
  617.2 5.7 fusion.16
  626.6 5.3 copy.22
  631.9 4.8 select_select_fusion
  636.8 103.3 %all-reduce.6.cloned.1.call-done = f32[4,512,512]{2,1,0:T(8,128)} async-done(((f32[4,512,512]{2,1,0:T(8,128)}), f32[4,512,512]{2,1,0:T(8,128)}) %all-reduce.6.cloned.1.call-update) | async-done | bytes 4194320 | tf_op jit(solution)/shard_map/psum | solution.py:13
  742.6 36.9 %reduce-scatter.5.cloned.1.call-done = f32[256,512]{1,0:T(8,128)} async-done(((f32[2048,512]{1,0:T(8,128)}), f32[256,512]{1,0:T(8,128)}) %reduce-scatter.5.cloned.1.call-update) | async-done | bytes 524304 | tf_op jit(solution)/shard_map/reduce_scatter | solution.py:28
  779.5 6.8 select_dynamic-update-slice_fusion
  786.3 29.1 %all-gather.9.cloned.1.call-done = f32[2048,512]{1,0:T(8,128)} async-done(((f32[256,512]{1,0:T(8,128)}), f32[2048,512]{1,0:T(8,128)}) %all-gather.9.cloned.1.call-update) | async-done | bytes 4194320 | tf_op jit(solution)/shard_map/all_gather | solution.py:29
  815.5 17.0 %fusion = f32[4,512,2,512]{3,1,2,0:T(8,128)S(1)} fusion(f32[4,512,512]{2,1,0:T(8,128)} %all-reduce.6.cloned.1.call-done, f32[2,2,512,512]{3,2,1,0:T(8,128)} %bitcast.194, s32[]{:T(128)S(6)} %select_n.187), kind=kOutput, calls=%fused_computation.7 | convolution fusion | flops 12884901888 | bytes 14680068 | tf_op jit(solution)/shard_map/dot_general | solution.py:37
  832.5 18.1 %subtract_subtract_fusion = f32[4,512,2,512]{3,1,2,0:T(8,128)} fusion(f32[4,512,2,512]{3,1,2,0:T(8,128)S(1)} %fusion, f32[4,512,2,512]{3,1,2,0:T(8,128)S(1)} %copy-done, f32[4,512,512]{2,1,0:T(8,128)S(1)} %copy-done.1, f32[2,2,512,512]{3,2,1,0:T(8,128)} %bitcast.193, s32[]{:T(128)S(6)} %select_n.187, pred[2]{0:T(512)(128)(4,1)S(1)} %iota_compare_fusion.3), kind=kOutput, calls=%fused_computation.4 | convolution fusion | flops 12889620480 | bytes 31457286 | tf_op jit(solution)/shard_map/dot_general | solution.py:37
  850.6 15.4 %copy.15 = f32[4,512,2,512]{3,2,1,0:T(2,128)} copy(f32[4,512,2,512]{3,1,2,0:T(8,128)} %subtract_subtract_fusion) | data formatting | bytes 16777216 | tf_op jit(solution)/shard_map/sub | solution.py:44
  (111 shorter events, 54.3 us)
Async XLA Ops:
  6.5 142.9 %all-gather.11.cloned.1.call-start = ((), (), s32[]{:S(2)}) async-start(), calls=%async_computation.8 | async-start | bytes 9437184 | tf_op jit(solution)/shard_map/all_gather | solution.py:8
  96.0 236.8 %all-reduce.4.cloned.1.call-start = ((), (), s32[]{:S(2)}) async-start(), calls=%async_computation.2 | async-start | bytes 8388608 | tf_op jit(solution)/shard_map/psum | solution.py:13
  198.9 6.6 copy-start.3
  229.4 142.7 %reduce-scatter.3.cloned.1.call-start = ((), (), s32[]{:S(2)}) async-start(), calls=%async_computation.3 | async-start | bytes 4718592 | tf_op jit(solution)/shard_map/reduce_scatter | solution.py:28
  335.3 72.8 %all-gather.7.cloned.1.call-start = ((), (), s32[]{:S(2)}) async-start(), calls=%async_computation.4 | async-start | bytes 4718592 | tf_op jit(solution)/shard_map/all_gather | solution.py:29
  372.2 185.1 %all-gather.13.cloned.1.call-start = ((), (), s32[]{:S(2)}) async-start(), calls=%async_computation.9 | async-start | bytes 9437184 | tf_op jit(solution)/shard_map/all_gather | solution.py:8
  507.6 232.5 %all-reduce.6.cloned.1.call-start = ((), (), s32[]{:S(2)}) async-start(), calls=%async_computation.5 | async-start | bytes 8388608 | tf_op jit(solution)/shard_map/psum | solution.py:13
  606.0 6.6 copy-start.2
  636.8 142.7 %reduce-scatter.5.cloned.1.call-start = ((), (), s32[]{:S(2)}) async-start(), calls=%async_computation.6 | async-start | bytes 4718592 | tf_op jit(solution)/shard_map/reduce_scatter | solution.py:28
  742.5 72.9 %all-gather.9.cloned.1.call-start = ((), (), s32[]{:S(2)}) async-start(), calls=%async_computation.7 | async-start | bytes 4718592 | tf_op jit(solution)/shard_map/all_gather | solution.py:29
  815.5 17.0 %copy-start = (f32[4,512,2,512]{3,1,2,0:T(8,128)S(1)}, f32[4,512,2,512]{3,1,2,0:T(8,128)}, u32[]{:S(2)}) copy-start(f32[4,512,2,512]{3,1,2,0:T(8,128)} %select_dynamic-update-slice_fusion) | copy-start | bytes 25165828
  815.5 17.0 %copy-start.1 = (f32[4,512,512]{2,1,0:T(8,128)S(1)}, f32[4,512,512]{2,1,0:T(8,128)}, u32[]{:S(2)}) copy-start(f32[4,512,512]{2,1,0:T(8,128)} %all-reduce.4.cloned.1.call-done) | copy-start | bytes 12582916
Sparse Core Ops, SparseCore 0:
  96.1 53.2 all-gather.10
  229.5 103.1 all-reduce.3
  335.4 36.7 reduce-scatter.2
  373.7 34.2 all-gather.6
  507.7 49.6 all-gather.12
  636.9 103.1 all-reduce.5
  742.7 36.7 reduce-scatter.4
  781.2 34.2 all-gather.8
where the time goes:
time: 883 us; the launch traced here: 873 us
  waiting for transfers between devices  419 us (47%)
  other arithmetic  278 us (31%)
  matrix products  85.5 us (10%)
  local copies, waits for them, and re-layouts  69.8 us (8%)
  between operations  20.2 us (2%)
    psum x2, waiting for transfers between devices, from_root(): return lax.psum(kept, axis)  207 us
    another operation x29, other arithmetic, factor_panel(): factor = picked(jnp.linalg.cholesky(diag_raw), 'row', owner_row)  158 us
    all_gather x2, waiting for transfers between devices, picked(): lax.all_gather(x, axis)  85.5 us
    another operation x5, other arithmetic, factor_panel(): jax.scipy.linalg.solve_triangular(factor, flat_rows.T, lower=True)  82 us
    reduce_scatter x2, waiting for transfers between devices, broadcast_by_parts(): own = lax.psum_scatter(padded, axis, scatter_dimension=0, tiled=True)  73.7 us
    all_gather x2, waiting for transfers between devices, broadcast_by_parts(): lax.all_gather(own, axis, axis=0, tiled=True)[:len(lines)].reshape(x.shape)  53.5 us
    another operation x14, matrix products, factor_panel(): jax.scipy.linalg.solve_triangular(factor, flat_rows.T, lower=True)  35.7 us
    dot_general x2, matrix products, update(): lax.dot_general(left_panel, right_panel, (((1,), (1,)), ((), ())), precis...  35.1 us
  transfers between devices with their start and end apart: 8, of which 8 were waited for; matrix products, arithmetic and copies ran while one was open for 4% of the time, Pallas kernels for 0%

commit v1 on v0

--- a/solution.py
+++ b/solution.py
@@ -26,7 +26,12 @@
     )
     padded = padded_to(lines, lax.axis_size(axis))
     own = lax.psum_scatter(padded, axis, scatter_dimension=0, tiled=True)
-    return lax.all_gather(own, axis, axis=0, tiled=True)[: len(lines)].reshape(x.shape)
+    return jnp.concatenate(
+        lax.all_to_all(
+            jnp.stack(lax.axis_size(axis) * [own]), axis_name=axis, split_axis=0, concat_axis=0
+        ),
+        axis=0,
+    )[: len(lines)].reshape(x.shape)
 
 
 def update(matrix, rows_part, cols_part):

time: 883 us -> 932 us (1.055)
  waiting for transfers between devices: 419 us -> 445 us
  starting transfers between devices: 0.29 us -> 16.2 us
    all_to_all x0 -> x2, waiting for transfers between devices: none -> 79.3 us  [broadcast_by_parts(): lax.all_to_all(jnp.stack(lax.axis_size(axis) * [own]), axis_name=axis, sp...]
    all_gather x2 -> x0, waiting for transfers between devices: 53.5 us -> none  [broadcast_by_parts(): lax.all_gather(own, axis, axis=0, tiled=True)[:len(lines)].reshape(x.shape)]
    all_to_all x0 -> x2, starting transfers between devices: none -> 16 us  [broadcast_by_parts(): lax.all_to_all(jnp.stack(lax.axis_size(axis) * [own]), axis_name=axis, sp...]
where the time goes in v1:
time: 932 us; the launch traced here: 922 us
  waiting for transfers between devices  445 us (48%)
  other arithmetic  277 us (30%)
  matrix products  85.5 us (9%)
  local copies, waits for them, and re-layouts  77.3 us (8%)
  between operations  20 us (2%)
  starting transfers between devices  16.2 us (2%)
    psum x2, waiting for transfers between devices, from_root(): return lax.psum(kept, axis)  207 us
    another operation x29, other arithmetic, factor_panel(): factor = picked(jnp.linalg.cholesky(diag_raw), 'row', owner_row)  158 us
    all_gather x2, waiting for transfers between devices, picked(): lax.all_gather(x, axis)  85.7 us
    another operation x5, other arithmetic, factor_panel(): jax.scipy.linalg.solve_triangular(factor, flat_rows.T, lower=True)  81.8 us
    all_to_all x2, waiting for transfers between devices, broadcast_by_parts(): lax.all_to_all(jnp.stack(lax.axis_size(axis) * [own]), axis_name=axis, sp...  79.3 us
    reduce_scatter x2, waiting for transfers between devices, broadcast_by_parts(): own = lax.psum_scatter(padded, axis, scatter_dimension=0, tiled=True)  73.8 us
    another operation x14, matrix products, factor_panel(): jax.scipy.linalg.solve_triangular(factor, flat_rows.T, lower=True)  35.5 us
    dot_general x2, matrix products, update(): lax.dot_general(left_panel, right_panel, (((1,), (1,)), ((), ())), precis...  35.1 us
  transfers between devices with their start and end apart: 8, of which 8 were waited for; matrix products, arithmetic and copies ran while one was open for 4% of the time, Pallas kernels for 0%

profile of v1, /device:TPU:1, one launch (start us, length us, event | category | flops | bytes accessed | tf_op | source)
XLA Modules:
  0.0 921.7 jit_solution(13470864316961851794)
XLA Ops:
  11.3 11.7 %cholesky.286 = f32[128,128]{1,0:T(8,128)S(1)} custom-call(f32[128,128]{1,0:T(8,128)S(1)} %cholesky.426), custom_call_target="Cholesky" | custom-call | tf_op jit(solution)/shard_map/jit(cholesky)/cholesky | solution.py:65
  23.1 9.8 %custom-call.27 = f32[1,128,128]{1,2,0:T(8,128)S(1)} custom-call(f32[1,128,128]{2,1,0:T(8,128)S(1)} %get-tuple-element.66), custom_call_target="InvertDiagBlocksLowerTriangular" | custom-call | tf_op jit(solution)/shard_map/jit(cholesky)/cholesky | solution.py:65
  33.7 11.7 %cholesky.305 = f32[128,128]{1,0:T(8,128)S(1)} custom-call(f32[128,128]{1,0:T(8,128)S(1)} %cholesky.430), custom_call_target="Cholesky" | custom-call | tf_op jit(solution)/shard_map/jit(cholesky)/cholesky | solution.py:65
  45.4 10.1 %custom-call.28 = f32[1,128,128]{1,2,0:T(8,128)S(1)} custom-call(f32[1,128,128]{2,1,0:T(8,128)S(1)} %get-tuple-element.63), custom_call_target="InvertDiagBlocksLowerTriangular" | custom-call | tf_op jit(solution)/shard_map/jit(cholesky)/cholesky | solution.py:65
  56.2 11.7 %cholesky.326 = f32[128,128]{1,0:T(8,128)S(1)} custom-call(f32[128,128]{1,0:T(8,128)S(1)} %cholesky.435), custom_call_target="Cholesky" | custom-call | tf_op jit(solution)/shard_map/jit(cholesky)/cholesky | solution.py:65
  68.6 9.8 %custom-call.29 = f32[1,128,128]{1,2,0:T(8,128)S(1)} custom-call(f32[1,128,128]{2,1,0:T(8,128)S(1)} %get-tuple-element.60), custom_call_target="InvertDiagBlocksLowerTriangular" | custom-call | tf_op jit(solution)/shard_map/jit(cholesky)/cholesky | solution.py:65
  79.0 11.7 %cholesky.343 = f32[128,128]{1,0:T(8,128)S(1)} custom-call(f32[128,128]{1,0:T(8,128)S(1)} %convolution_subtract_fusion.9), custom_call_target="Cholesky" | custom-call | tf_op jit(solution)/shard_map/jit(cholesky)/cholesky | solution.py:65
  95.8 8.3 copy.19
  104.1 4.6 constant_dynamic-slice_fusion.5
  108.7 40.5 %all-gather.5.cloned.1.call-done = f32[4096,512]{1,0:T(8,128)} async-done(((f32[512,512]{1,0:T(8,128)}), f32[4096,512]{1,0:T(8,128)}) %all-gather.5.cloned.1.call-update) | async-done | bytes 8388624 | tf_op jit(solution)/shard_map/all_gather | solution.py:8
  150.7 8.2 while.4
  158.9 39.5 %custom-call.30 = f32[4,128,128]{1,2,0:T(8,128)S(1)} custom-call(f32[4,128,128]{2,1,0:T(8,128)S(1)} %get-tuple-element.21), custom_call_target="InvertDiagBlocksLowerTriangular" | custom-call | tf_op jit(solution)/shard_map/jit(_solve_triangular)/triangular_solve | solution.py:67
  205.0 3.5 convolution_subtract_fusion.1
  209.6 5.6 fusion.19
  218.7 5.3 copy.30
  224.0 4.9 select_select_fusion.1
  229.0 103.3 %all-reduce.4.cloned.1.call-done = f32[4,512,512]{2,1,0:T(8,128)} async-done(((f32[4,512,512]{2,1,0:T(8,128)}), f32[4,512,512]{2,1,0:T(8,128)}) %all-reduce.4.cloned.1.call-update) | async-done | bytes 4194320 | tf_op jit(solution)/shard_map/psum | solution.py:13
  334.7 36.9 %reduce-scatter.3.cloned.1.call-done = f32[256,512]{1,0:T(8,128)} async-done(((f32[2048,512]{1,0:T(8,128)}), f32[256,512]{1,0:T(8,128)}) %reduce-scatter.3.cloned.1.call-update) | async-done | bytes 524304 | tf_op jit(solution)/shard_map/reduce_scatter | solution.py:28
  371.6 3.5 stack.4
  375.1 8.0 all-to-all-start
  383.2 6.8 select_dynamic-update-slice_fusion.1
  390.0 4.6 constant_dynamic-slice_fusion.4
  394.6 37.3 %all-to-all-done = f32[8,256,512]{2,1,0:T(8,128)} async-done(((f32[8,256,512]{2,1,0:T(8,128)}), f32[8,256,512]{2,1,0:T(8,128)}, u32[]{:S(2)}, u32[]{:S(2)}) %all-to-all-start) | async-done | bytes 4194336 | tf_op jit(solution)/shard_map/all_to_all | solution.py:30
  432.0 11.1 %bitcast_dynamic-update-slice_fusion.2 = f32[4,512,2,512]{3,1,2,0:T(8,128)} fusion(f32[4,512,2,512]{3,1,2,0:T(8,128)} %select_dynamic-update-slice_fusion.1, s32[]{:T(128)S(6)} %select_n.178, f32[4,512,1,512]{3,1,2,0:T(8,128)} %constant_dynamic-slice_fusion.4, f32[4,512,512]{2,1,0:T(8,128)} %all-reduce.4.cloned.1.call-done, ...), kind=kOutput, calls=%fused_computation.11 | convolution fusion | flops 6443499520 | bytes 13631500 | tf_op jit(solution)/shard_map/dot_general | solution.py:97
  446.2 11.7 %cholesky.358 = f32[128,128]{1,0:T(8,128)S(1)} custom-call(f32[128,128]{1,0:T(8,128)S(1)} %cholesky.439), custom_call_target="Cholesky" | custom-call | tf_op jit(solution)/shard_map/jit(cholesky)/cholesky | solution.py:65
  458.6 9.8 %custom-call.31 = f32[1,128,128]{1,2,0:T(8,128)S(1)} custom-call(f32[1,128,128]{2,1,0:T(8,128)S(1)} %get-tuple-element.56), custom_call_target="InvertDiagBlocksLowerTriangular" | custom-call | tf_op jit(solution)/shard_map/jit(cholesky)/cholesky | solution.py:65
  469.2 11.7 %cholesky.377 = f32[128,128]{1,0:T(8,128)S(1)} custom-call(f32[128,128]{1,0:T(8,128)S(1)} %cholesky.443), custom_call_target="Cholesky" | custom-call | tf_op jit(solution)/shard_map/jit(cholesky)/cholesky | solution.py:65
  481.6 9.9 %custom-call.32 = f32[1,128,128]{1,2,0:T(8,128)S(1)} custom-call(f32[1,128,128]{2,1,0:T(8,128)S(1)} %get-tuple-element.53), custom_call_target="InvertDiagBlocksLowerTriangular" | custom-call | tf_op jit(solution)/shard_map/jit(cholesky)/cholesky | solution.py:65
  492.3 11.7 %cholesky.398 = f32[128,128]{1,0:T(8,128)S(1)} custom-call(f32[128,128]{1,0:T(8,128)S(1)} %cholesky.448), custom_call_target="Cholesky" | custom-call | tf_op jit(solution)/shard_map/jit(cholesky)/cholesky | solution.py:65
  504.7 9.8 %custom-call.33 = f32[1,128,128]{1,2,0:T(8,128)S(1)} custom-call(f32[1,128,128]{2,1,0:T(8,128)S(1)} %get-tuple-element.50), custom_call_target="InvertDiagBlocksLowerTriangular" | custom-call | tf_op jit(solution)/shard_map/jit(cholesky)/cholesky | solution.py:65
  515.1 11.7 %cholesky.415 = f32[128,128]{1,0:T(8,128)S(1)} custom-call(f32[128,128]{1,0:T(8,128)S(1)} %convolution_subtract_fusion.8), custom_call_target="Cholesky" | custom-call | tf_op jit(solution)/shard_map/jit(cholesky)/cholesky | solution.py:65
  531.4 4.6 constant_dynamic-slice_fusion.2
  536.0 45.3 %all-gather.7.cloned.1.call-done = f32[4096,512]{1,0:T(8,128)} async-done(((f32[512,512]{1,0:T(8,128)}), f32[4096,512]{1,0:T(8,128)}) %all-gather.7.cloned.1.call-update) | async-done | bytes 8388624 | tf_op jit(solution)/shard_map/all_gather | solution.py:8
  582.8 8.3 while.5
  591.1 39.3 %custom-call.34 = f32[4,128,128]{1,2,0:T(8,128)S(1)} custom-call(f32[4,128,128]{2,1,0:T(8,128)S(1)} %get-tuple-element.22), custom_call_target="InvertDiagBlocksLowerTriangular" | custom-call | tf_op jit(solution)/shard_map/jit(_solve_triangular)/triangular_solve | solution.py:67
  637.0 3.5 convolution_subtract_fusion
  641.7 5.5 fusion.16
  650.7 5.3 copy.33
  656.1 4.8 select_select_fusion
  661.0 103.3 %all-reduce.6.cloned.1.call-done = f32[4,512,512]{2,1,0:T(8,128)} async-done(((f32[4,512,512]{2,1,0:T(8,128)}), f32[4,512,512]{2,1,0:T(8,128)}) %all-reduce.6.cloned.1.call-update) | async-done | bytes 4194320 | tf_op jit(solution)/shard_map/psum | solution.py:13
  766.7 36.9 %reduce-scatter.5.cloned.1.call-done = f32[256,512]{1,0:T(8,128)} async-done(((f32[2048,512]{1,0:T(8,128)}), f32[256,512]{1,0:T(8,128)}) %reduce-scatter.5.cloned.1.call-update) | async-done | bytes 524304 | tf_op jit(solution)/shard_map/reduce_scatter | solution.py:28
  803.6 3.5 stack.5
  807.2 8.0 all-to-all-start.1
  815.2 6.8 select_dynamic-update-slice_fusion
  822.1 41.9 %all-to-all-done.1 = f32[8,256,512]{2,1,0:T(8,128)} async-done(((f32[8,256,512]{2,1,0:T(8,128)}), f32[8,256,512]{2,1,0:T(8,128)}, u32[]{:S(2)}, u32[]{:S(2)}) %all-to-all-start.1) | async-done | bytes 4194336 | tf_op jit(solution)/shard_map/all_to_all | solution.py:30
  864.0 17.0 %fusion = f32[4,512,2,512]{3,1,2,0:T(8,128)S(1)} fusion(f32[4,512,512]{2,1,0:T(8,128)} %all-reduce.6.cloned.1.call-done, f32[2,2,512,512]{3,2,1,0:T(8,128)} %bitcast.57, s32[]{:T(128)S(6)} %select_n.187), kind=kOutput, calls=%fused_computation.7 | convolution fusion | flops 12884901888 | bytes 14680068 | tf_op jit(solution)/shard_map/dot_general | solution.py:42
  881.0 18.1 %subtract_subtract_fusion = f32[4,512,2,512]{3,1,2,0:T(8,128)} fusion(f32[4,512,2,512]{3,1,2,0:T(8,128)S(1)} %fusion, f32[4,512,2,512]{3,1,2,0:T(8,128)S(1)} %copy-done, f32[4,512,512]{2,1,0:T(8,128)S(1)} %copy-done.1, f32[2,2,512,512]{3,2,1,0:T(8,128)} %bitcast.24, s32[]{:T(128)S(6)} %select_n.187, pred[2]{0:T(512)(128)(4,1)S(1)} %iota_compare_fusion.3), kind=kOutput, calls=%fused_computation.4 | convolution fusion | flops 12889620480 | bytes 31457286 | tf_op jit(solution)/shard_map/dot_general | solution.py:42
  899.1 15.4 %copy.26 = f32[4,512,2,512]{3,2,1,0:T(2,128)} copy(f32[4,512,2,512]{3,1,2,0:T(8,128)} %subtract_subtract_fusion) | data formatting | bytes 16777216 | tf_op jit(solution)/shard_map/sub | solution.py:49
  (111 shorter events, 65.4 us)
Async XLA Ops:
  6.5 142.6 %all-gather.5.cloned.1.call-start = ((), (), s32[]{:S(2)}) async-start(), calls=%async_computation.8 | async-start | bytes 9437184 | tf_op jit(solution)/shard_map/all_gather | solution.py:8
  95.7 236.5 %all-reduce.4.cloned.1.call-start = ((), (), s32[]{:S(2)}) async-start(), calls=%async_computation.4 | async-start | bytes 8388608 | tf_op jit(solution)/shard_map/psum | solution.py:13
  198.4 6.6 copy-start.3
  228.9 142.7 %reduce-scatter.3.cloned.1.call-start = ((), (), s32[]{:S(2)}) async-start(), calls=%async_computation.5 | async-start | bytes 4718592 | tf_op jit(solution)/shard_map/reduce_scatter | solution.py:28
  375.1 56.8 %all-to-all-start = ((f32[8,256,512]{2,1,0:T(8,128)}), f32[8,256,512]{2,1,0:T(8,128)}, u32[]{:S(2)}, u32[]{:S(2)}) async-start(f32[8,256,512]{2,1,0:T(8,128)} %stack.4), calls=%async_computation.1 | async-start | bytes 8388608 | tf_op jit(solution)/shard_map/all_to_all | solution.py:30
  383.1 198.2 %all-gather.7.cloned.1.call-start = ((), (), s32[]{:S(2)}) async-start(), calls=%async_computation.9 | async-start | bytes 9437184 | tf_op jit(solution)/shard_map/all_gather | solution.py:8
  531.3 232.9 %all-reduce.6.cloned.1.call-start = ((), (), s32[]{:S(2)}) async-start(), calls=%async_computation.6 | async-start | bytes 8388608 | tf_op jit(solution)/shard_map/psum | solution.py:13
  630.4 6.6 copy-start.2
  660.9 142.7 %reduce-scatter.5.cloned.1.call-start = ((), (), s32[]{:S(2)}) async-start(), calls=%async_computation.7 | async-start | bytes 4718592 | tf_op jit(solution)/shard_map/reduce_scatter | solution.py:28
  807.2 56.8 %all-to-all-start.1 = ((f32[8,256,512]{2,1,0:T(8,128)}), f32[8,256,512]{2,1,0:T(8,128)}, u32[]{:S(2)}, u32[]{:S(2)}) async-start(f32[8,256,512]{2,1,0:T(8,128)} %stack.5), calls=%async_computation.3 | async-start | bytes 8388608 | tf_op jit(solution)/shard_map/all_to_all | solution.py:30
  864.0 17.0 %copy-start = (f32[4,512,2,512]{3,1,2,0:T(8,128)S(1)}, f32[4,512,2,512]{3,1,2,0:T(8,128)}, u32[]{:S(2)}) copy-start(f32[4,512,2,512]{3,1,2,0:T(8,128)} %select_dynamic-update-slice_fusion) | copy-start | bytes 25165828
  864.0 17.0 %copy-start.1 = (f32[4,512,512]{2,1,0:T(8,128)S(1)}, f32[4,512,512]{2,1,0:T(8,128)}, u32[]{:S(2)}) copy-start(f32[4,512,512]{2,1,0:T(8,128)} %all-reduce.4.cloned.1.call-done) | copy-start | bytes 12582916
Sparse Core Ops, SparseCore 0:
  95.9 53.2 all-gather.4
  229.0 103.1 all-reduce.3
  334.8 36.7 reduce-scatter.2
  531.4 49.8 all-gather.6
  661.1 103.1 all-reduce.5
  766.9 36.7 reduce-scatter.4
